TPU v7x, 32 devices: a whole 2x2x4 slice. The times are simulated.
32 devices in a mesh: sib: 4 (over y, x), wide: 8 (over z, core).
Axes of the slice: x: 2, y: 2, z: 4, core: 2. Of those that a mesh axis runs over, the one named last changes fastest.
Arguments:
- right_side: float32 [128, 8, 2048], P(None, 'wide', 'sib'), may hold values from -6 to 6
- tree_order: int32 [8, 2048], P('wide', 'sib'), may hold values from 0 to 2047, each once within a row
- x_start: float32 [128, 8, 2048], P(None, 'wide', 'sib'), may hold values from -6 to 6
- tangent_start: float32 [128, 8, 2048], P(None, 'wide', 'sib'), may hold values from -3 to 3
- dense_kernel: float32 [8, 4, 512, 512], P('wide', 'sib'), may hold values from -0.25 to 0.25
- dense_deriv: float32 [8, 4, 512, 512], P('wide', 'sib'), may hold values from -0.25 to 0.25
- leaf_basis: float32 [8, 4, 512, 256], P('wide', 'sib'), may hold values from -0.25 to 0.25
- transfer: float32 [8, 4, 256, 256], P('wide', 'sib'), may hold values from -0.375 to 0.375
- sibling_kernel: float32 [8, 4, 3, 256, 256], P('wide', 'sib'), may hold values from -0.21875 to 0.21875
- sibling_deriv: float32 [8, 4, 3, 256, 256], P('wide', 'sib'), may hold values from -0.21875 to 0.21875
- partner_list: int32 [8, 4], P('wide'), may hold values from 0 to 7, as said below
- parent_kernel: float32 [8, 4, 256, 256], P('wide'), may hold values from -0.1875 to 0.1875
- parent_deriv: float32 [8, 4, 256, 256], P('wide'), may hold values from -0.1875 to 0.1875
Outputs:
- solution: float32 [128, 8, 2048], P(None, 'wide', 'sib')
- tangent: float32 [128, 8, 2048], P(None, 'wide', 'sib')
Inputs may be any that keep to these rules, and one draw needn't show every extreme that they name: `partner_list`: row p names 4 different parent clusters, none of them p. `tree_order`: each row holds every position 0 .. 2047 once.
All inputs are finite; a program needn't handle non-finite values.
Results may differ from a plain program's by a relative error of at most 0.0001.
Values sent between devices are 32-bit elements; how exact they have to be, the bound alone decides.
No kernel may reach another device: no remote copies, remote signals or barrier semaphores. Data moves between devices by JAX's collectives and lax.ppermute only.
A program may use at most 64 MiB of HBM per device.

v0:
```python
import jax
import jax.numpy as jnp
from jax import lax
from jax.sharding import PartitionSpec as P

ITERS = 2
highest = lax.Precision.HIGHEST
relax_step = 0.3
noise_level = 1.0


def product(left, right):
    return jnp.dot(left, right, precision=highest, preferred_element_type=jnp.float32)


def product_t(left, right):
    return lax.dot_general(
        left, right, (((1,), (1,)), ((), ())), precision=highest, preferred_element_type=jnp.float32
    )


def body(
    right_side,
    tree_order,
    x_start,
    tangent_start,
    dense_kernel,
    dense_deriv,
    leaf_basis,
    transfer,
    sibling_kernel,
    sibling_deriv,
    partner_list,
    parent_kernel,
    parent_deriv,
):
    order = tree_order[0]
    dense = dense_kernel[0, 0]
    dense_d = dense_deriv[0, 0]
    basis = leaf_basis[0, 0]
    trans = transfer[0, 0]
    sib_k = sibling_kernel[0, 0]
    sib_d = sibling_deriv[0, 0]
    partners = partner_list[0]
    par_k = parent_kernel[0]
    par_d = parent_deriv[0]
    me = lax.axis_index("sib")
    count = lax.axis_size("sib")
    piece = lax.all_gather(right_side, "sib", axis=2, tiled=True)
    rows = piece.shape[2]
    inside = (order >= 0) & (order < rows)
    taken = jnp.take(piece[:, 0, :], jnp.clip(order, 0, rows - 1), axis=1)
    rhs = jnp.where(inside[None, :], taken, 0.0)
    x = x_start[:, 0, :]
    dx = tangent_start[:, 0, :]
    for step in range(ITERS):
        coeff_x = product(x, basis)
        coeff_dx = product(dx, basis)
        empty = jnp.zeros(coeff_x.shape, jnp.float32)
        term_x = product(coeff_x, trans)
        term_dx = product(coeff_dx, trans)
        start = jnp.int32(0)
        add_field_x = empty
        add_field_dx = empty
        add_piece_x = lax.all_gather(coeff_x[None], "sib", axis=0, tiled=True)
        add_piece_dx = lax.all_gather(coeff_dx[None], "sib", axis=0, tiled=True)
        for item in range(add_piece_x.shape[0]):
            other = start + item
            slot = jnp.clip((other - me - 1 + count) % count, 0, count - 2)
            weight = jnp.where(other == me, 0.0, 1.0).astype(jnp.float32)
            kern = lax.dynamic_index_in_dim(sib_k, slot, 0, keepdims=False)
            deriv = lax.dynamic_index_in_dim(sib_d, slot, 0, keepdims=False)
            add_field_x = add_field_x + weight * product(add_piece_x[item], kern)
            add_field_dx = add_field_dx + weight * (
                product(add_piece_x[item], deriv) + product(add_piece_dx[item], kern)
            )
        upper_x, upper_dx = (
            lax.psum_scatter(term_x, "sib", scatter_dimension=0, tiled=True),
            lax.psum_scatter(term_dx, "sib", scatter_dimension=0, tiled=True),
        )
        piece_x = lax.all_gather(upper_x[None], "wide", axis=0, tiled=True)
        piece_dx = lax.all_gather(upper_dx[None], "wide", axis=0, tiled=True)
        index = jnp.arange(piece_x.shape[0], dtype=jnp.int32)
        select = (index[None, :] == partners[:, None]).astype(jnp.float32)
        chosen_x = jnp.einsum(
            "bn,nrk->brk", select, piece_x, precision=highest, preferred_element_type=jnp.float32
        )
        chosen_dx = jnp.einsum(
            "bn,nrk->brk", select, piece_dx, precision=highest, preferred_element_type=jnp.float32
        )
        field_x = jnp.einsum(
            "brk,bkm->rm", chosen_x, par_k, precision=highest, preferred_element_type=jnp.float32
        )
        field_dx = jnp.einsum(
            "brk,bkm->rm", chosen_x, par_d, precision=highest, preferred_element_type=jnp.float32
        ) + jnp.einsum(
            "brk,bkm->rm", chosen_dx, par_k, precision=highest, preferred_element_type=jnp.float32
        )
        far_x, far_dx = (
            lax.all_gather(field_x, "sib", axis=0, tiled=True),
            lax.all_gather(field_dx, "sib", axis=0, tiled=True),
        )
        down_x = add_field_x + product_t(far_x, trans)
        down_dx = add_field_dx + product_t(far_dx, trans)
        image = product(x, dense) + product_t(down_x, basis)
        dimage = product(x, dense_d) + product(dx, dense) + product_t(down_dx, basis)
        x_next = x + relax_step * (rhs - noise_level * x - image)
        dx = dx - relax_step * (noise_level * dx + dimage)
        x = x_next
    return (x[:, None, :], dx[:, None, :])


def solution(mesh):
    placed = (
        P(None, "wide", "sib"),
        P("wide", "sib"),
        P(None, "wide", "sib"),
        P(None, "wide", "sib"),
        P("wide", "sib", None, None),
        P("wide", "sib", None, None),
        P("wide", "sib", None, None),
        P("wide", "sib", None, None),
        P("wide", "sib", None, None, None),
        P("wide", "sib", None, None, None),
        P("wide", None),
        P("wide", None, None, None),
        P("wide", None, None, None),
    )
    return jax.shard_map(
        body,
        mesh=mesh,
        in_specs=placed,
        out_specs=(P(None, "wide", "sib"), P(None, "wide", "sib")),
        check_vma=False,
    )
```

profile of v0, /device:TPU:0, one launch (start us, length us, event | category | flops | bytes accessed | tf_op | source)
XLA Modules:
  0.0 240.8 jit_solution(12168629055974303689)
XLA Ops:
  7.2 1.6 fusion.62
  8.9 0.9 fusion.95
  10.3 0.9 fusion.89
  11.4 12.0 %all-gather = f32[512,256]{1,0:T(8,128)S(1)} all-gather(f32[128,256]{1,0:T(8,128)S(1)} %fusion.62), channel_id=2, replica_groups=mesh['sib'=4,'wide'=8] {'sib'}, dimensions={0}, use_global_device_ids=true | all-gather | bytes 655360 | tf_op jit(solution)/shard_map/all_gather | solution.py:65
  23.4 11.2 %all-gather.4 = f32[512,256]{1,0:T(8,128)} all-gather(f32[128,256]{1,0:T(8,128)S(1)} %fusion.56), channel_id=6, replica_groups=mesh['sib'=4,'wide'=8] {'sib'}, dimensions={0}, use_global_device_ids=true | all-gather | bytes 655360 | tf_op jit(solution)/shard_map/all_gather | solution.py:66
  34.9 0.9 fusion.79
  35.8 0.9 fusion.75
  36.8 0.9 fusion.71
  37.7 2.0 fusion.40
  39.7 1.4 convolution_add_fusion.5
  43.9 0.9 fusion.22
  44.8 14.7 %all-gather.1 = f32[256,256]{1,0:T(8,128)S(1)} all-gather(f32[32,256]{1,0:T(8,128)} %reduce-scatter.5.cloned.1.call-done), channel_id=3, replica_groups=mesh['sib'=4,'wide'=8] {'wide'}, dimensions={0}, use_global_device_ids=true | all-gather | bytes 294912 | tf_op jit(solution)/shard_map/all_gather | solution.py:81
  59.5 0.7 copy-done.34
  60.6 4.5 %reduce-scatter.9.cloned.1.call-done = f32[32,256]{1,0:T(8,128)} async-done(((f32[128,256]{1,0:T(8,128)}), f32[32,256]{1,0:T(8,128)}) %reduce-scatter.9.cloned.1.call-update) | async-done | bytes 32784 | tf_op jit(solution)/shard_map/reduce_scatter | solution.py:79
  65.2 14.6 %all-gather.5 = f32[256,256]{1,0:T(8,128)S(1)} all-gather(f32[32,256]{1,0:T(8,128)} %reduce-scatter.9.cloned.1.call-done), channel_id=7, replica_groups=mesh['sib'=4,'wide'=8] {'wide'}, dimensions={0}, use_global_device_ids=true | all-gather | bytes 294912 | tf_op jit(solution)/shard_map/all_gather | solution.py:82
  80.1 1.8 convolution_bitcast_fusion.3
  82.6 8.6 %all_gather.48 = f32[128,256]{1,0:T(8,128)S(1)} all-gather(f32[32,256]{1,0:T(8,128)S(1)} %fusion.35), channel_id=1, replica_groups=mesh['sib'=4,'wide'=8] {'sib'}, dimensions={0}, use_global_device_ids=true | all-gather | bytes 163840 | tf_op jit(solution)/shard_map/all_gather | solution.py:101
  92.2 0.6 fusion.8
  93.6 0.6 copy-done.20
  94.2 0.9 fusion.86
  95.2 1.8 copy.21
  98.7 1.4 fusion.50
  100.7 7.8 %all_gather.42 = f32[128,256]{1,0:T(8,128)S(1)} all-gather(f32[32,256]{1,0:T(8,128)S(1)} %convolution_bitcast_fusion.5), channel_id=1, replica_groups=mesh['sib'=4,'wide'=8] {'sib'}, dimensions={0}, use_global_device_ids=true | all-gather | bytes 163840 | tf_op jit(solution)/shard_map/all_gather | solution.py:100
  108.5 10.8 %all-gather.6 = f32[512,256]{1,0:T(8,128)} all-gather(f32[128,256]{1,0:T(8,128)S(1)} %copy-done.21), channel_id=8, replica_groups=mesh['sib'=4,'wide'=8] {'sib'}, dimensions={0}, use_global_device_ids=true | all-gather | bytes 655360 | tf_op jit(solution)/shard_map/all_gather | solution.py:66
  119.7 14.5 %all-gather.7 = f32[256,256]{1,0:T(8,128)S(1)} all-gather(f32[32,256]{1,0:T(8,128)} %reduce-scatter.11.cloned.1.call-done), channel_id=9, replica_groups=mesh['sib'=4,'wide'=8] {'wide'}, dimensions={0}, use_global_device_ids=true | all-gather | bytes 294912 | tf_op jit(solution)/shard_map/all_gather | solution.py:82
  134.2 1.1 fusion.113
  135.3 13.0 %all-gather.10.cloned.1.call-done = f32[128,1,2048]{0,2,1:T(8,128)} async-done(((f32[128,1,512]{0,2,1:T(8,128)}), f32[128,1,2048]{0,2,1:T(8,128)}) %all-gather.10.cloned.1.call-update) | async-done | bytes 1048592 | tf_op jit(solution)/shard_map/all_gather | solution.py:49
  148.3 2.3 gather_fusion
  150.7 1.7 fusion.13
  152.8 0.9 fusion.92
  153.7 10.2 %all-gather.2 = f32[512,256]{1,0:T(8,128)S(1)} all-gather(f32[128,256]{1,0:T(8,128)S(1)} %fusion.59), channel_id=4, replica_groups=mesh['sib'=4,'wide'=8] {'sib'}, dimensions={0}, use_global_device_ids=true | all-gather | bytes 655360 | tf_op jit(solution)/shard_map/all_gather | solution.py:65
  163.9 2.0 fusion.81
  165.9 0.9 fusion.77
  166.8 0.9 fusion.73
  167.8 0.9 fusion.69
  168.7 1.4 fusion.38
  170.4 2.5 %convolution_add_fusion.4 = f32[128,512]{1,0:T(8,128)} fusion(f32[128,512]{1,0:T(8,128)} %fusion.38, f32[128,512]{1,0:T(8,128)} %copy-done.10, f32[1,1,512,512]{3,2,1,0:T(8,128)S(1)} %copy-done), kind=kOutput, calls=%fused_computation.19 | convolution fusion | flops 402718720 | bytes 1835008 | tf_op jit(solution)/shard_map/dot_general | solution.py:13
  176.6 0.6 copy-done.27
  177.5 0.7 fusion.48
  178.2 16.5 %reduce-scatter.7.cloned.1.call-done = f32[32,256]{1,0:T(8,128)} async-done(((f32[128,256]{1,0:T(8,128)}), f32[32,256]{1,0:T(8,128)}) %reduce-scatter.7.cloned.1.call-update) | async-done | bytes 32784 | tf_op jit(solution)/shard_map/reduce_scatter | solution.py:78
  194.7 14.6 %all-gather.3 = f32[256,256]{1,0:T(8,128)S(1)} all-gather(f32[32,256]{1,0:T(8,128)} %reduce-scatter.7.cloned.1.call-done), channel_id=5, replica_groups=mesh['sib'=4,'wide'=8] {'wide'}, dimensions={0}, use_global_device_ids=true | all-gather | bytes 294912 | tf_op jit(solution)/shard_map/all_gather | solution.py:81
  209.7 1.8 convolution_bitcast_fusion.1
  213.1 8.4 %all_gather.51 = f32[128,256]{1,0:T(8,128)S(1)} all-gather(f32[32,256]{1,0:T(8,128)S(1)} %fusion.34), channel_id=1, replica_groups=mesh['sib'=4,'wide'=8] {'sib'}, dimensions={0}, use_global_device_ids=true | all-gather | bytes 163840 | tf_op jit(solution)/shard_map/all_gather | solution.py:101
  222.5 0.6 fusion.6
  223.2 1.0 copy.26
  224.1 7.5 %all_gather.45 = f32[128,256]{1,0:T(8,128)S(1)} all-gather(f32[32,256]{1,0:T(8,128)S(1)} %convolution_bitcast_fusion.4), channel_id=1, replica_groups=mesh['sib'=4,'wide'=8] {'sib'}, dimensions={0}, use_global_device_ids=true | all-gather | bytes 163840 | tf_op jit(solution)/shard_map/all_gather | solution.py:100
  232.6 0.7 fusion.11
  233.3 1.0 copy.25
  (115 shorter events, 18.0 us)
Async XLA Ops:
  7.2 32.5 %copy-start = (f32[1,1,512,512]{3,2,1,0:T(8,128)S(1)}, f32[1,1,512,512]{3,2,1,0:T(8,128)}, u32[]{:S(2)}) copy-start(f32[1,1,512,512]{3,2,1,0:T(8,128)} %param.17) | copy-start | bytes 3145732
  7.2 1.7 copy-start.3
  7.2 37.6 %reduce-scatter.5.cloned.1.call-start = ((), (), s32[]{:S(2)}) async-start(), calls=%async_computation.5 | async-start | bytes 163840 | tf_op jit(solution)/shard_map/reduce_scatter | solution.py:78
  7.2 2.7 %copy-start.13 = (f32[128,1,512]{2,1,0:T(1,128)S(1)}, f32[128,1,512]{2,1,0:T(1,128)}, u32[]{:S(2)}) copy-start(f32[128,1,512]{2,1,0:T(1,128)} %param.16) | copy-start | bytes 786436
  8.9 1.0 copy-start.1
  9.9 55.3 %reduce-scatter.9.cloned.1.call-start = ((), (), s32[]{:S(2)}) async-start(), calls=%async_computation.7 | async-start | bytes 163840 | tf_op jit(solution)/shard_map/reduce_scatter | solution.py:79
  11.3 23.3 %copy-start.7 = (f32[1,1,3,256,256]{4,3,2,1,0:T(8,128)S(1)}, f32[1,1,3,256,256]{4,3,2,1,0:T(8,128)}, u32[]{:S(2)}) copy-start(f32[1,1,3,256,256]{4,3,2,1,0:T(8,128)} %param.22) | copy-start | bytes 2359300
  11.3 108.4 %reduce-scatter.11.cloned.1.call-start = ((), (), s32[]{:S(2)}) async-start(), calls=%async_computation.8 | async-start | bytes 163840 | tf_op jit(solution)/shard_map/reduce_scatter | solution.py:79
  36.7 1.0 copy-start.12
  37.7 2.0 copy-start.14
  39.7 1.4 copy-start.2
  39.7 1.4 copy-start.18
  41.2 0.9 copy-start.26
  42.1 0.9 copy-start.29
  43.0 0.9 copy-start.32
  59.5 0.7 copy-start.34
  65.2 16.8 %copy-start.4 = (f32[1,4,256,256]{3,2,1,0:T(8,128)S(1)}, f32[1,4,256,256]{3,2,1,0:T(8,128)}, u32[]{:S(2)}) copy-start(f32[1,4,256,256]{3,2,1,0:T(8,128)} %param.24) | copy-start | bytes 3145732
  82.6 8.6 %copy-start.30 = (f32[128,256]{1,0:T(8,128)S(1)}, f32[128,256]{1,0:T(8,128)}, u32[]{:S(2)}) copy-start(f32[128,256]{1,0:T(8,128)} %fusion.22) | copy-start | bytes 393220
  91.2 1.0 copy-start.15
  91.2 1.0 copy-start.23
  92.8 0.7 copy-start.10
  93.6 0.6 copy-start.20
  95.2 53.1 %all-gather.10.cloned.1.call-start = ((), (), s32[]{:S(2)}) async-start(), calls=%async_computation.4 | async-start | bytes 1310720 | tf_op jit(solution)/shard_map/all_gather | solution.py:49
  97.0 0.7 copy-start.33
  97.0 97.7 %reduce-scatter.7.cloned.1.call-start = ((), (), s32[]{:S(2)}) async-start(), calls=%async_computation.6 | async-start | bytes 163840 | tf_op jit(solution)/shard_map/reduce_scatter | solution.py:78
  98.4 1.7 copy-start.5
  100.7 7.8 %copy-start.21 = (f32[128,256]{1,0:T(8,128)S(1)}, f32[128,256]{1,0:T(8,128)}, u32[]{:S(2)}) copy-start(f32[128,256]{1,0:T(8,128)} %copy-done.20) | copy-start | bytes 393220
  150.7 1.7 copy-start.16
  153.7 12.2 %copy-start.8 = (f32[1,1,3,256,256]{4,3,2,1,0:T(8,128)S(1)}, f32[1,1,3,256,256]{4,3,2,1,0:T(8,128)}, u32[]{:S(2)}) copy-start(f32[1,1,3,256,256]{4,3,2,1,0:T(8,128)} %param.22) | copy-start | bytes 2359300
  163.9 4.8 %copy-start.9 = (f32[1,1,512,512]{3,2,1,0:T(8,128)S(1)}, f32[1,1,512,512]{3,2,1,0:T(8,128)}, u32[]{:S(2)}) copy-start(f32[1,1,512,512]{3,2,1,0:T(8,128)} %param.18) | copy-start | bytes 3145732
  173.2 1.0 copy-start.19
  173.5 0.9 copy-start.24
  174.5 0.9 copy-start.31
  175.4 0.9 copy-start.28
  176.3 0.9 copy-start.27
  194.7 16.8 %copy-start.6 = (f32[1,4,256,256]{3,2,1,0:T(8,128)S(1)}, f32[1,4,256,256]{3,2,1,0:T(8,128)}, u32[]{:S(2)}) copy-start(f32[1,4,256,256]{3,2,1,0:T(8,128)} %param.24) | copy-start | bytes 3145732
  211.6 0.9 copy-start.25
  221.5 1.0 copy-start.11
  221.5 1.0 copy-start.22
  231.7 1.0 copy-start.17
Sparse Core Ops, SparseCore 0:
  11.3 26.8 reduce-scatter.4
  41.0 24.1 reduce-scatter.8
  95.3 24.0 reduce-scatter.10
  121.7 26.5 all-gather.9
  170.6 24.1 reduce-scatter.6
where the time goes:
time: 242 us; the launch traced here: 241 us
  blocking collectives  135 us (56%)
  matrix products  42.6 us (18%)
  waiting for transfers between devices  34.2 us (14%)
  local copies, waits for them, and re-layouts  14.5 us (6%)
  between operations  14.4 us (6%)
    all_gather x2, blocking collectives, body(): piece_x = lax.all_gather(upper_x[None], 'wide', axis=0, tiled=True)  29.3 us
    dot_general x38, matrix products, product(): jnp.dot(left, right, precision=highest, preferred_element_type=jnp.float32)  29.1 us
    all_gather x2, blocking collectives, body(): piece_dx = lax.all_gather(upper_dx[None], 'wide', axis=0, tiled=True)  29.1 us
    all_gather x2, blocking collectives, body(): add_piece_x = lax.all_gather(coeff_x[None], 'sib', axis=0, tiled=True)  22.2 us
    all_gather x2, blocking collectives, body(): add_piece_dx = lax.all_gather(coeff_dx[None], 'sib', axis=0, tiled=True)  22 us
    all_gather x2, blocking collectives, body(): lax.all_gather(field_dx, 'sib', axis=0, tiled=True)  17 us
    reduce_scatter x2, waiting for transfers between devices, body(): lax.psum_scatter(term_x, 'sib', scatter_dimension=0, tiled=True)  16.5 us
    all_gather x2, blocking collectives, body(): lax.all_gather(field_x, 'sib', axis=0, tiled=True)  15.3 us
  transfers between devices with their start and end apart: 5, of which 3 were waited for; matrix products, arithmetic and copies ran while one was open for 9% of the time, Pallas kernels for 0%

commit v1 on v0

--- a/solution.py
+++ b/solution.py
@@ -7,6 +7,22 @@
 highest = lax.Precision.HIGHEST
 relax_step = 0.3
 noise_level = 1.0
+
+
+def product_in_turn(x, axis, dim, product):
+    size, place, extent = (lax.axis_size(axis), lax.axis_index(axis), x.shape[dim])
+    ahead = [(i, (i + 1) % size) for i in range(size)]
+    left = [(i, (i - 1) % size) for i in range(size)]
+    middle = size // 2
+    from_left = from_right = x
+    running = product(x, place * extent)
+    for step in range(1, middle + 1):
+        from_left = lax.ppermute(from_left, axis, ahead)
+        if step < size - middle:
+            from_right = lax.ppermute(from_right, axis, left)
+            running = running + product(from_right, (place + step) % size * extent)
+        running = running + product(from_left, (place - step) % size * extent)
+    return running
 
 
 def product(left, right):
@@ -79,14 +95,22 @@
             lax.psum_scatter(term_dx, "sib", scatter_dimension=0, tiled=True),
         )
         piece_x = lax.all_gather(upper_x[None], "wide", axis=0, tiled=True)
-        piece_dx = lax.all_gather(upper_dx[None], "wide", axis=0, tiled=True)
         index = jnp.arange(piece_x.shape[0], dtype=jnp.int32)
         select = (index[None, :] == partners[:, None]).astype(jnp.float32)
         chosen_x = jnp.einsum(
             "bn,nrk->brk", select, piece_x, precision=highest, preferred_element_type=jnp.float32
         )
-        chosen_dx = jnp.einsum(
-            "bn,nrk->brk", select, piece_dx, precision=highest, preferred_element_type=jnp.float32
+        chosen_dx = product_in_turn(
+            upper_dx[None],
+            "wide",
+            0,
+            lambda part, start_2: jnp.einsum(
+                "bn,nrk->brk",
+                lax.dynamic_slice_in_dim(select, start_2, part.shape[0], axis=1),
+                part,
+                precision=highest,
+                preferred_element_type=jnp.float32,
+            ),
         )
         field_x = jnp.einsum(
             "brk,bkm->rm", chosen_x, par_k, precision=highest, preferred_element_type=jnp.float32

time: 242 us -> 257 us (1.062)
  blocking collectives: 135 us -> 109 us
  starting transfers between devices: 0.21 us -> 17.1 us
  waiting for transfers between devices: 34.2 us -> 49.9 us
  matrix products: 42.6 us -> 47.1 us
    all_gather x2 -> x0, blocking collectives: 29.1 us -> none  [body(): piece_dx = lax.all_gather(upper_dx[None], 'wide', axis=0, tiled=True)]
    ppermute x0 -> x14, starting transfers between devices: none -> 16.9 us  [the longest x6 16.9 us: product_in_turn(): from_right = lax.ppermute(from_right, axis, left)]
    all_gather x1, waiting for transfers between devices: 13 us -> 0.01 us  [body(): piece = lax.all_gather(right_side, 'sib', axis=2, tiled=True)]
    reduce_scatter x2, waiting for transfers between devices: 16.5 us -> 28.4 us  [body(): lax.psum_scatter(term_x, 'sib', scatter_dimension=0, tiled=True)]
    reduce_scatter x2, waiting for transfers between devices: 4.57 us -> 14.8 us  [body(): lax.psum_scatter(term_dx, 'sib', scatter_dimension=0, tiled=True)]
    ppermute x0 -> x14, waiting for transfers between devices: none -> 6.62 us  [the longest x8 4.79 us: product_in_turn(): from_left = lax.ppermute(from_left, axis, ahead)]
    unnamed x73 -> x125, local copies, waits for them, and re-layouts: 12.1 us -> 13.7 us
  transfers between devices with their start and end apart: 5 -> 19, of which waited for: 3 -> 8; matrix products, arithmetic and copies ran while one was open for 9% -> 17% of each run, Pallas kernels for 0% -> 0%
where the time goes in v1:
time: 257 us; the launch traced here: 256 us
  blocking collectives  109 us (42%)
  waiting for transfers between devices  49.9 us (19%)
  matrix products  47.1 us (18%)
  starting transfers between devices  17.1 us (7%)
  local copies, waits for them, and re-layouts  16.8 us (7%)
  between operations  14.7 us (6%)
    dot_general x38, matrix products, product(): jnp.dot(left, right, precision=highest, preferred_element_type=jnp.float32)  31.5 us
    all_gather x2, blocking collectives, body(): piece_x = lax.all_gather(upper_x[None], 'wide', axis=0, tiled=True)  29.1 us
    reduce_scatter x2, waiting for transfers between devices, body(): lax.psum_scatter(term_x, 'sib', scatter_dimension=0, tiled=True)  28.4 us
    all_gather x2, blocking collectives, body(): add_piece_dx = lax.all_gather(coeff_dx[None], 'sib', axis=0, tiled=True)  23.8 us
    all_gather x2, blocking collectives, body(): add_piece_x = lax.all_gather(coeff_x[None], 'sib', axis=0, tiled=True)  22.8 us
    all_gather x2, blocking collectives, body(): lax.all_gather(field_dx, 'sib', axis=0, tiled=True)  17.1 us
    ppermute x6, starting transfers between devices, product_in_turn(): from_right = lax.ppermute(from_right, axis, left)  16.9 us
    all_gather x2, blocking collectives, body(): lax.all_gather(field_x, 'sib', axis=0, tiled=True)  16.2 us
  transfers between devices with their start and end apart: 19, of which 8 were waited for; matrix products, arithmetic and copies ran while one was open for 17% of the time, Pallas kernels for 0%

profile of v1, /device:TPU:0, one launch (start us, length us, event | category | flops | bytes accessed | tf_op | source)
XLA Modules:
  0.0 256.3 jit_solution(2117172351519161854)
XLA Ops:
  7.2 1.6 fusion.56
  12.2 12.3 %all-gather = f32[512,256]{1,0:T(8,128)S(1)} all-gather(f32[128,256]{1,0:T(8,128)} %copy-done.18), channel_id=2, replica_groups=mesh['sib'=4,'wide'=8] {'sib'}, dimensions={0}, use_global_device_ids=true | all-gather | bytes 655360 | tf_op jit(solution)/shard_map/all_gather | solution.py:81
  24.5 10.2 %all-gather.4 = f32[512,256]{1,0:T(8,128)} all-gather(f32[128,256]{1,0:T(8,128)S(1)} %fusion.56), channel_id=6, replica_groups=mesh['sib'=4,'wide'=8] {'sib'}, dimensions={0}, use_global_device_ids=true | all-gather | bytes 655360 | tf_op jit(solution)/shard_map/all_gather | solution.py:82
  35.0 1.0 fusion.79
  35.9 0.9 fusion.75
  36.9 0.9 fusion.71
  37.8 2.6 %fusion.40 = f32[128,512]{1,0:T(8,128)} fusion(f32[1,1,512,512]{3,2,1,0:T(8,128)} %param.18, f32[128,1,512]{2,1,0:T(1,128)S(1)} %copy-done.11), kind=kOutput, calls=%fused_computation.73 | convolution fusion | flops 402653184 | bytes 1572864 | tf_op jit(solution)/shard_map/dot_general | solution.py:29
  40.5 2.5 convolution_add_fusion.5
  47.9 3.5 %collective-permute-start = (f32[1,32,256]{2,1,0:T(8,128)}, f32[1,32,256]{2,1,0:T(8,128)}, u32[]{:S(2)}, u32[]{:S(2)}) collective-permute-start(f32[1,32,256]{2,1,0:T(8,128)} %bitcast.227), channel_id=1, source_target_pairs={{0,7},{1,0},{2,1},{3,2},{4,3},{5,4},{6,5},{7,6},{8,15},{9,8},{10,9... | collective-permute-start | bytes 98312 | tf_op jit(solution)/shard_map/ppermute | solution.py:22
  51.5 1.2 collective-permute-done.1
  52.7 12.5 %reduce-scatter.5.cloned.1.call-done = f32[32,256]{1,0:T(8,128)} async-done(((f32[128,256]{1,0:T(8,128)}), f32[32,256]{1,0:T(8,128)}) %reduce-scatter.5.cloned.1.call-update) | async-done | bytes 32784 | tf_op jit(solution)/shard_map/reduce_scatter | solution.py:94
  65.2 14.6 %all-gather.1 = f32[256,256]{1,0:T(8,128)S(1)} all-gather(f32[32,256]{1,0:T(8,128)} %reduce-scatter.5.cloned.1.call-done), channel_id=3, replica_groups=mesh['sib'=4,'wide'=8] {'wide'}, dimensions={0}, use_global_device_ids=true | all-gather | bytes 294912 | tf_op jit(solution)/shard_map/all_gather | solution.py:97
  79.7 3.3 %collective-permute-start.2 = (f32[1,32,256]{2,1,0:T(8,128)}, f32[1,32,256]{2,1,0:T(8,128)S(1)}, u32[]{:S(2)}, u32[]{:S(2)}) collective-permute-start(f32[1,32,256]{2,1,0:T(8,128)} %collective-permute-done), channel_id=1, source_target_pairs={{0,7},{1,0},{2,1},{3,2},{4,3},{5,4},{6,5},{7,6},{8,15},{9,8},{10,9... | collective-permute-start | bytes 98312 | tf_op jit(solution)/shard_map/ppermute | solution.py:22
  83.0 1.1 fusion.115
  84.9 3.4 %collective-permute-start.4 = (f32[1,32,256]{2,1,0:T(8,128)S(1)}, f32[1,32,256]{2,1,0:T(8,128)S(1)}, u32[]{:S(2)}, u32[]{:S(2)}) collective-permute-start(f32[1,32,256]{2,1,0:T(8,128)S(1)} %collective-permute-done.2), channel_id=1, source_target_pairs={{0,7},{1,0},{2,1},{3,2},{4,3},{5,4},{6,5},{7,6},{8,15},{9,8},{10,9... | collective-permute-start | bytes 98312 | tf_op jit(solution)/shard_map/ppermute | solution.py:22
  88.7 1.8 convolution_bitcast_fusion.3
  90.5 3.3 %collective-permute-done.6 = f32[1,32,256]{2,1,0:T(8,128)S(1)} collective-permute-done((f32[1,32,256]{2,1,0:T(8,128)S(1)}, f32[1,32,256]{2,1,0:T(8,128)S(1)}, u32[]{:S(2)}, u32[]{:S(2)}) %collective-permute-start.6) | collective-permute-done | bytes 32800 | tf_op jit(solution)/shard_map/ppermute | solution.py:20
  94.4 1.4 fusion.35
  95.9 8.5 %all_gather.41 = f32[128,256]{1,0:T(8,128)S(1)} all-gather(f32[32,256]{1,0:T(8,128)S(1)} %fusion.35), channel_id=1, replica_groups=mesh['sib'=4,'wide'=8] {'sib'}, dimensions={0}, use_global_device_ids=true | all-gather | bytes 163840 | tf_op jit(solution)/shard_map/all_gather | solution.py:125
  108.2 1.8 copy.23
  112.5 0.9 fusion.31
  113.4 1.4 fusion.50
  114.8 14.8 %reduce-scatter.11.cloned.1.call-done = f32[32,256]{1,0:T(8,128)} async-done(((f32[128,256]{1,0:T(8,128)}), f32[32,256]{1,0:T(8,128)}) %reduce-scatter.11.cloned.1.call-update) | async-done | bytes 32784 | tf_op jit(solution)/shard_map/reduce_scatter | solution.py:95
  129.7 1.8 convolution_bitcast_fusion.5
  131.5 8.7 %all_gather.36 = f32[128,256]{1,0:T(8,128)S(1)} all-gather(f32[32,256]{1,0:T(8,128)S(1)} %convolution_bitcast_fusion.5), channel_id=1, replica_groups=mesh['sib'=4,'wide'=8] {'sib'}, dimensions={0}, use_global_device_ids=true | all-gather | bytes 163840 | tf_op jit(solution)/shard_map/all_gather | solution.py:124
  140.2 1.5 collective-permute-start.7
  142.3 1.0 collective-permute-done.7
  143.2 3.5 %collective-permute-start.9 = (f32[1,32,256]{2,1,0:T(8,128)S(1)}, f32[1,32,256]{2,1,0:T(8,128)}, u32[]{:S(2)}, u32[]{:S(2)}) collective-permute-start(f32[1,32,256]{2,1,0:T(8,128)S(1)} %collective-permute-done.7), channel_id=1, source_target_pairs={{0,7},{1,0},{2,1},{3,2},{4,3},{5,4},{6,5},{7,6},{8,15},{9,8},{10,9... | collective-permute-start | bytes 98312 | tf_op jit(solution)/shard_map/ppermute | solution.py:22
  146.8 13.7 %all-gather.5 = f32[512,256]{1,0:T(8,128)} all-gather(f32[128,256]{1,0:T(8,128)S(1)} %copy-done.20), channel_id=7, replica_groups=mesh['sib'=4,'wide'=8] {'sib'}, dimensions={0}, use_global_device_ids=true | all-gather | bytes 655360 | tf_op jit(solution)/shard_map/all_gather | solution.py:82
  160.5 1.6 collective-permute-start.11
  162.1 2.3 gather_fusion
  165.3 1.7 fusion.13
  168.4 10.5 %all-gather.2 = f32[512,256]{1,0:T(8,128)S(1)} all-gather(f32[128,256]{1,0:T(8,128)S(1)} %fusion.59), channel_id=4, replica_groups=mesh['sib'=4,'wide'=8] {'sib'}, dimensions={0}, use_global_device_ids=true | all-gather | bytes 655360 | tf_op jit(solution)/shard_map/all_gather | solution.py:81
  178.9 2.1 fusion.81
  181.0 0.9 fusion.77
  181.9 0.9 fusion.73
  182.9 0.9 fusion.69
  184.9 1.4 convolution_add_fusion.4
  190.6 0.9 fusion.15
  191.5 1.4 fusion.48
  193.0 15.9 %reduce-scatter.7.cloned.1.call-done = f32[32,256]{1,0:T(8,128)} async-done(((f32[128,256]{1,0:T(8,128)}), f32[32,256]{1,0:T(8,128)}) %reduce-scatter.7.cloned.1.call-update) | async-done | bytes 32784 | tf_op jit(solution)/shard_map/reduce_scatter | solution.py:94
  208.9 14.5 %all-gather.3 = f32[256,256]{1,0:T(8,128)S(1)} all-gather(f32[32,256]{1,0:T(8,128)} %reduce-scatter.7.cloned.1.call-done), channel_id=5, replica_groups=mesh['sib'=4,'wide'=8] {'wide'}, dimensions={0}, use_global_device_ids=true | all-gather | bytes 294912 | tf_op jit(solution)/shard_map/all_gather | solution.py:97
  223.8 1.8 convolution_bitcast_fusion.1
  226.9 1.5 fusion.34
  228.4 8.5 %all_gather.43 = f32[128,256]{1,0:T(8,128)S(1)} all-gather(f32[32,256]{1,0:T(8,128)S(1)} %fusion.34), channel_id=1, replica_groups=mesh['sib'=4,'wide'=8] {'sib'}, dimensions={0}, use_global_device_ids=true | all-gather | bytes 163840 | tf_op jit(solution)/shard_map/all_gather | solution.py:125
  238.5 1.0 copy.30
  239.5 7.5 %all_gather.39 = f32[128,256]{1,0:T(8,128)S(1)} all-gather(f32[32,256]{1,0:T(8,128)S(1)} %convolution_bitcast_fusion.4), channel_id=1, replica_groups=mesh['sib'=4,'wide'=8] {'sib'}, dimensions={0}, use_global_device_ids=true | all-gather | bytes 163840 | tf_op jit(solution)/shard_map/all_gather | solution.py:124
  248.8 1.0 copy.29
  (193 shorter events, 29.2 us)
Async XLA Ops:
  7.2 33.3 %copy-start = (f32[1,1,512,512]{3,2,1,0:T(8,128)S(1)}, f32[1,1,512,512]{3,2,1,0:T(8,128)}, u32[]{:S(2)}) copy-start(f32[1,1,512,512]{3,2,1,0:T(8,128)} %param.17) | copy-start | bytes 3145732
  7.2 1.7 copy-start.3
  7.2 40.1 %reduce-scatter.9.cloned.1.call-start = ((), (), s32[]{:S(2)}) async-start(), calls=%async_computation.7 | async-start | bytes 163840 | tf_op jit(solution)/shard_map/reduce_scatter | solution.py:95
  7.2 2.7 %copy-start.11 = (f32[128,1,512]{2,1,0:T(1,128)S(1)}, f32[128,1,512]{2,1,0:T(1,128)}, u32[]{:S(2)}) copy-start(f32[128,1,512]{2,1,0:T(1,128)} %param.15) | copy-start | bytes 786436
  8.9 1.0 copy-start.1
  9.9 55.3 %reduce-scatter.5.cloned.1.call-start = ((), (), s32[]{:S(2)}) async-start(), calls=%async_computation.5 | async-start | bytes 163840 | tf_op jit(solution)/shard_map/reduce_scatter | solution.py:94
  12.0 117.7 %reduce-scatter.11.cloned.1.call-start = ((), (), s32[]{:S(2)}) async-start(), calls=%async_computation.8 | async-start | bytes 163840 | tf_op jit(solution)/shard_map/reduce_scatter | solution.py:95
  12.0 22.6 %copy-start.6 = (f32[1,1,3,256,256]{4,3,2,1,0:T(8,128)S(1)}, f32[1,1,3,256,256]{4,3,2,1,0:T(8,128)}, u32[]{:S(2)}) copy-start(f32[1,1,3,256,256]{4,3,2,1,0:T(8,128)} %param.22) | copy-start | bytes 2359300
  40.5 2.6 copy-start.2
  40.5 2.6 copy-start.16
  47.3 5.3 %collective-permute-start.1 = (f32[1,32,256]{2,1,0:T(8,128)}, f32[1,32,256]{2,1,0:T(8,128)S(1)}, u32[]{:S(2)}, u32[]{:S(2)}) collective-permute-start(f32[1,32,256]{2,1,0:T(8,128)} %bitcast.226), channel_id=1, source_target_pairs={{0,1},{1,2},{2,3},{3,4},{4,5},{5,6},{6,7},{7,0},{8,9},{9,10},{10,1... | collective-permute-start | bytes 98312 | tf_op jit(solution)/shard_map/ppermute | solution.py:20
  47.9 45.9 %copy-start.46 = (f32[4]{0:T(128)}, f32[4]{0:T(128)S(1)}, u32[]{:S(2)}) copy-start(f32[4]{0:T(128)S(1)} %get-tuple-element.9) | copy-start | bytes 52
  47.9 31.8 %collective-permute-start = (f32[1,32,256]{2,1,0:T(8,128)}, f32[1,32,256]{2,1,0:T(8,128)}, u32[]{:S(2)}, u32[]{:S(2)}) collective-permute-start(f32[1,32,256]{2,1,0:T(8,128)} %bitcast.227), channel_id=1, source_target_pairs={{0,7},{1,0},{2,1},{3,2},{4,3},{5,4},{6,5},{7,6},{8,15},{9,8},{10,9... | collective-permute-start | bytes 98312 | tf_op jit(solution)/shard_map/ppermute | solution.py:22
  52.7 27.1 %copy-start.43 = (f32[1,32,256]{2,1,0:T(8,128)}, f32[1,32,256]{2,1,0:T(8,128)S(1)}, u32[]{:S(2)}) copy-start(f32[1,32,256]{2,1,0:T(8,128)S(1)} %collective-permute-done.1) | copy-start | bytes 98308
  52.7 30.4 %collective-permute-start.3 = (f32[1,32,256]{2,1,0:T(8,128)S(1)}, f32[1,32,256]{2,1,0:T(8,128)}, u32[]{:S(2)}, u32[]{:S(2)}) collective-permute-start(f32[1,32,256]{2,1,0:T(8,128)S(1)} %collective-permute-done.1), channel_id=1, source_target_pairs={{0,1},{1,2},{2,3},{3,4},{4,5},{5,6},{6,7},{7,0},{8,9},{9,10},{10,1... | collective-permute-start | bytes 98312 | tf_op jit(solution)/shard_map/ppermute | solution.py:20
  65.2 28.6 %copy-start.4 = (f32[1,4,256,256]{3,2,1,0:T(8,128)S(1)}, f32[1,4,256,256]{3,2,1,0:T(8,128)}, u32[]{:S(2)}) copy-start(f32[1,4,256,256]{3,2,1,0:T(8,128)} %param.24) | copy-start | bytes 3145732
  79.7 5.2 %collective-permute-start.2 = (f32[1,32,256]{2,1,0:T(8,128)}, f32[1,32,256]{2,1,0:T(8,128)S(1)}, u32[]{:S(2)}, u32[]{:S(2)}) collective-permute-start(f32[1,32,256]{2,1,0:T(8,128)} %collective-permute-done), channel_id=1, source_target_pairs={{0,7},{1,0},{2,1},{3,2},{4,3},{5,4},{6,5},{7,6},{8,15},{9,8},{10,9... | collective-permute-start | bytes 98312 | tf_op jit(solution)/shard_map/ppermute | solution.py:22
  83.0 5.6 %collective-permute-start.5 = (f32[1,32,256]{2,1,0:T(8,128)}, f32[1,32,256]{2,1,0:T(8,128)S(1)}, u32[]{:S(2)}, u32[]{:S(2)}) collective-permute-start(f32[1,32,256]{2,1,0:T(8,128)} %collective-permute-done.3), channel_id=1, source_target_pairs={{0,1},{1,2},{2,3},{3,4},{4,5},{5,6},{6,7},{7,0},{8,9},{9,10},{10,1... | collective-permute-start | bytes 98312 | tf_op jit(solution)/shard_map/ppermute | solution.py:20
  84.9 5.5 %collective-permute-start.4 = (f32[1,32,256]{2,1,0:T(8,128)S(1)}, f32[1,32,256]{2,1,0:T(8,128)S(1)}, u32[]{:S(2)}, u32[]{:S(2)}) collective-permute-start(f32[1,32,256]{2,1,0:T(8,128)S(1)} %collective-permute-done.2), channel_id=1, source_target_pairs={{0,7},{1,0},{2,1},{3,2},{4,3},{5,4},{6,5},{7,6},{8,15},{9,8},{10,9... | collective-permute-start | bytes 98312 | tf_op jit(solution)/shard_map/ppermute | solution.py:22
  88.6 5.1 %collective-permute-start.6 = (f32[1,32,256]{2,1,0:T(8,128)S(1)}, f32[1,32,256]{2,1,0:T(8,128)S(1)}, u32[]{:S(2)}, u32[]{:S(2)}) collective-permute-start(f32[1,32,256]{2,1,0:T(8,128)S(1)} %collective-permute-done.5), channel_id=1, source_target_pairs={{0,1},{1,2},{2,3},{3,4},{4,5},{5,6},{6,7},{7,0},{8,9},{9,10},{10,1... | collective-permute-start | bytes 98312 | tf_op jit(solution)/shard_map/ppermute | solution.py:20
  88.6 5.2 %copy-start.34 = (f32[32,256]{1,0:T(8,128)S(1)}, f32[32,256]{1,0:T(8,128)}, u32[]{:S(2)}) copy-start(f32[32,256]{1,0:T(8,128)} %reduce-scatter.9.cloned.1.call-done) | copy-start | bytes 98308
  88.7 5.2 %copy-start.44 = (f32[1,32,256]{2,1,0:T(8,128)S(1)}, f32[1,32,256]{2,1,0:T(8,128)}, u32[]{:S(2)}) copy-start(f32[1,32,256]{2,1,0:T(8,128)} %copy-done.43) | copy-start | bytes 98308
  95.9 8.6 %copy-start.26 = (f32[128,256]{1,0:T(8,128)S(1)}, f32[128,256]{1,0:T(8,128)}, u32[]{:S(2)}) copy-start(f32[128,256]{1,0:T(8,128)} %fusion.22) | copy-start | bytes 393220
  104.5 1.0 copy-start.21
  108.1 54.0 %all-gather.8.cloned.1.call-start = ((), (), s32[]{:S(2)}) async-start(), calls=%async_computation.4 | async-start | bytes 1310720 | tf_op jit(solution)/shard_map/all_gather | solution.py:65
  110.0 98.8 %reduce-scatter.7.cloned.1.call-start = ((), (), s32[]{:S(2)}) async-start(), calls=%async_computation.6 | async-start | bytes 163840 | tf_op jit(solution)/shard_map/reduce_scatter | solution.py:94
  129.7 12.0 %collective-permute-start.8 = (f32[1,32,256]{2,1,0:T(8,128)}, f32[1,32,256]{2,1,0:T(8,128)S(1)}, u32[]{:S(2)}, u32[]{:S(2)}) collective-permute-start(f32[1,32,256]{2,1,0:T(8,128)} %bitcast.228), channel_id=1, source_target_pairs={{0,1},{1,2},{2,3},{3,4},{4,5},{5,6},{6,7},{7,0},{8,9},{9,10},{10,1... | collective-permute-start | bytes 98312 | tf_op jit(solution)/shard_map/ppermute | solution.py:20
  131.5 8.7 %copy-start.35 = (f32[32,256]{1,0:T(8,128)S(1)}, f32[32,256]{1,0:T(8,128)}, u32[]{:S(2)}) copy-start(f32[32,256]{1,0:T(8,128)} %reduce-scatter.11.cloned.1.call-done) | copy-start | bytes 98308
  131.5 10.1 %copy-start.24 = (f32[128,256]{1,0:T(8,128)S(1)}, f32[128,256]{1,0:T(8,128)}, u32[]{:S(2)}) copy-start(f32[128,256]{1,0:T(8,128)} %fusion.31) | copy-start | bytes 393220
  140.2 6.6 %copy-start.20 = (f32[128,256]{1,0:T(8,128)S(1)}, f32[128,256]{1,0:T(8,128)}, u32[]{:S(2)}) copy-start(f32[128,256]{1,0:T(8,128)} %copy-done.19) | copy-start | bytes 393220
  140.2 3.1 %collective-permute-start.7 = (f32[1,32,256]{2,1,0:T(8,128)S(1)}, f32[1,32,256]{2,1,0:T(8,128)S(1)}, u32[]{:S(2)}, u32[]{:S(2)}) collective-permute-start(f32[1,32,256]{2,1,0:T(8,128)S(1)} %bitcast.229), channel_id=1, source_target_pairs={{0,7},{1,0},{2,1},{3,2},{4,3},{5,4},{6,5},{7,6},{8,15},{9,8},{10,9... | collective-permute-start | bytes 98312 | tf_op jit(solution)/shard_map/ppermute | solution.py:22
  141.6 5.1 %collective-permute-start.10 = (f32[1,32,256]{2,1,0:T(8,128)S(1)}, f32[1,32,256]{2,1,0:T(8,128)S(1)}, u32[]{:S(2)}, u32[]{:S(2)}) collective-permute-start(f32[1,32,256]{2,1,0:T(8,128)S(1)} %collective-permute-done.8), channel_id=1, source_target_pairs={{0,1},{1,2},{2,3},{3,4},{4,5},{5,6},{6,7},{7,0},{8,9},{9,10},{10,1... | collective-permute-start | bytes 98312 | tf_op jit(solution)/shard_map/ppermute | solution.py:20
  143.2 17.2 %copy-start.39 = (f32[1,32,256]{2,1,0:T(8,128)}, f32[1,32,256]{2,1,0:T(8,128)S(1)}, u32[]{:S(2)}) copy-start(f32[1,32,256]{2,1,0:T(8,128)S(1)} %collective-permute-done.7) | copy-start | bytes 98308
  143.2 17.2 %collective-permute-start.9 = (f32[1,32,256]{2,1,0:T(8,128)S(1)}, f32[1,32,256]{2,1,0:T(8,128)}, u32[]{:S(2)}, u32[]{:S(2)}) collective-permute-start(f32[1,32,256]{2,1,0:T(8,128)S(1)} %collective-permute-done.7), channel_id=1, source_target_pairs={{0,7},{1,0},{2,1},{3,2},{4,3},{5,4},{6,5},{7,6},{8,15},{9,8},{10,9... | collective-permute-start | bytes 98312 | tf_op jit(solution)/shard_map/ppermute | solution.py:22
  146.8 13.7 %copy-start.41 = (f32[1,32,256]{2,1,0:T(8,128)}, f32[1,32,256]{2,1,0:T(8,128)S(1)}, u32[]{:S(2)}) copy-start(f32[1,32,256]{2,1,0:T(8,128)S(1)} %collective-permute-done.10) | copy-start | bytes 98308
  146.8 15.3 %collective-permute-start.12 = (f32[1,32,256]{2,1,0:T(8,128)S(1)}, f32[1,32,256]{2,1,0:T(8,128)}, u32[]{:S(2)}, u32[]{:S(2)}) collective-permute-start(f32[1,32,256]{2,1,0:T(8,128)S(1)} %collective-permute-done.10), channel_id=1, source_target_pairs={{0,1},{1,2},{2,3},{3,4},{4,5},{5,6},{6,7},{7,0},{8,9},{9,10},{10,1... | collective-permute-start | bytes 98312 | tf_op jit(solution)/shard_map/ppermute | solution.py:20
  160.5 65.8 %collective-permute-start.11 = (f32[1,32,256]{2,1,0:T(8,128)}, f32[1,32,256]{2,1,0:T(8,128)}, u32[]{:S(2)}, u32[]{:S(2)}) collective-permute-start(f32[1,32,256]{2,1,0:T(8,128)} %collective-permute-done.9), channel_id=1, source_target_pairs={{0,7},{1,0},{2,1},{3,2},{4,3},{5,4},{6,5},{7,6},{8,15},{9,8},{10,9... | collective-permute-start | bytes 98312 | tf_op jit(solution)/shard_map/ppermute | solution.py:22
  162.1 64.2 %collective-permute-start.13 = (f32[1,32,256]{2,1,0:T(8,128)}, f32[1,32,256]{2,1,0:T(8,128)}, u32[]{:S(2)}, u32[]{:S(2)}) collective-permute-start(f32[1,32,256]{2,1,0:T(8,128)} %collective-permute-done.12), channel_id=1, source_target_pairs={{0,1},{1,2},{2,3},{3,4},{4,5},{5,6},{6,7},{7,0},{8,9},{9,10},{10,1... | collective-permute-start | bytes 98312 | tf_op jit(solution)/shard_map/ppermute | solution.py:20
  168.4 12.6 %copy-start.7 = (f32[1,1,3,256,256]{4,3,2,1,0:T(8,128)S(1)}, f32[1,1,3,256,256]{4,3,2,1,0:T(8,128)}, u32[]{:S(2)}) copy-start(f32[1,1,3,256,256]{4,3,2,1,0:T(8,128)} %param.22) | copy-start | bytes 2359300
  178.9 5.7 %copy-start.8 = (f32[512,256]{1,0:T(8,128)}, f32[512,256]{1,0:T(8,128)S(1)}, u32[]{:S(2)}) copy-start(f32[512,256]{1,0:T(8,128)S(1)} %all-gather.2) | copy-start | bytes 1572868
  178.9 5.0 %copy-start.10 = (f32[1,1,512,512]{3,2,1,0:T(8,128)S(1)}, f32[1,1,512,512]{3,2,1,0:T(8,128)}, u32[]{:S(2)}) copy-start(f32[1,1,512,512]{3,2,1,0:T(8,128)} %param.18) | copy-start | bytes 3145732
  184.9 1.4 copy-start.9
  186.6 1.0 copy-start.17
  191.5 31.9 %copy-start.60 = (s32[1,4]{1,0:T(1,128)S(1)}, s32[1,4]{1,0:T(1,128)}, u32[]{:S(2)}) copy-start(s32[1,4]{1,0:T(1,128)} %param.23) | copy-start | bytes 52
  193.0 32.7 %copy-start.5 = (f32[1,4,256,256]{3,2,1,0:T(8,128)S(1)}, f32[1,4,256,256]{3,2,1,0:T(8,128)}, u32[]{:S(2)}) copy-start(f32[1,4,256,256]{3,2,1,0:T(8,128)} %param.24) | copy-start | bytes 3145732
  228.4 8.5 %copy-start.30 = (f32[128,256]{1,0:T(8,128)S(1)}, f32[128,256]{1,0:T(8,128)}, u32[]{:S(2)}) copy-start(f32[128,256]{1,0:T(8,128)} %fusion.15) | copy-start | bytes 393220
  247.0 1.0 copy-start.23
  247.1 1.0 copy-start.57
  (32 other events, 25.5 us)
Sparse Core Ops, SparseCore 0:
  10.7 26.8 reduce-scatter.8
  41.0 24.1 reduce-scatter.4
  108.3 21.3 reduce-scatter.10
  131.9 29.3 all-gather.7
  185.0 23.8 reduce-scatter.6
